TPU v7x, 32 devices: a whole 2x2x4 slice. The times are simulated.
32 devices in a mesh: row: 4 (over y, core), col: 8 (over z, x).
Axes of the slice: x: 2, y: 2, z: 4, core: 2. Of those that a mesh axis runs over, the one named last changes fastest.
Arguments:
- hidden_acts: bfloat16 [256, 29568], P('row', 'col'), may hold values from -6 to 6
- output_errors: bfloat16 [256, 4096], P('col', 'row'), may hold values from -6 to 6
- col_points: int32 [8], replicated, may hold values from 0 to 16, as said below
- row_points: int32 [4], replicated, may hold values from 0 to 8, as said below
- worker_mask: int32 [4, 8], replicated, may hold values from 0 to 1, as said below
Outputs:
- clipped_grad: float32 [2, 2048, 29568], P(None, 'col', 'row')
Inputs may be any that keep to these rules, and one draw needn't show every extreme that they name: `col_points`: distinct node indices. `row_points`: distinct node indices. `worker_mask`: each row of the grid has between 1 and 2 erased workers.
All inputs are finite; a program needn't handle non-finite values.
Results may differ from a plain program's by a relative error of at most 0.02.
Values may be sent and summed in bfloat16 or wider, within the bound.
A program may use at most 192 MiB of HBM per device.

v0:
```python
import jax
import jax.numpy as jnp
from jax import lax
from jax.sharding import PartitionSpec as P

D = 4096
FF = 29568


def node_value(index, count):
    return jnp.cos(jnp.pi * (2.0 * index.astype(jnp.float32) + 1.0) / (2.0 * count))


def berrut(nodes, signs, live, targets):
    terms = (live * signs)[:, None] / (targets[None, :] - nodes[:, None])
    return terms / jnp.sum(terms, axis=0, keepdims=True)


def rank_signs(points, live):
    lower = (points[None, :] < points[:, None]).astype(jnp.int32)
    ranks = jnp.sum(lower * live[None, :], axis=1)
    return (1 - 2 * (ranks % 2)).astype(jnp.float32)


def encode_blocks(source, weights, block_count, block_width):

    def add_block(index, total):
        piece = lax.dynamic_slice_in_dim(source, index * block_width, block_width, 1).astype(
            jnp.float32
        )
        factor = lax.dynamic_slice_in_dim(weights, index, 1, 0)
        return total + factor * piece

    start = jnp.zeros((source.shape[0], block_width), jnp.float32)
    return lax.fori_loop(0, block_count, add_block, start).astype(jnp.bfloat16)


def shards(hidden_acts, output_errors, col_points, row_points, worker_mask):
    col_count = lax.axis_size("col")
    row_count = lax.axis_size("row")
    col_place = lax.axis_index("col")
    row_place = lax.axis_index("row")
    act_blocks = col_count // 2
    err_blocks = row_count // 2
    act_width = FF // act_blocks
    err_width = D // err_blocks
    data_acts = node_value(jnp.arange(act_blocks), act_blocks)
    data_errs = node_value(jnp.arange(err_blocks), err_blocks)
    work_acts = node_value(col_points, 2 * col_count + 1)
    work_errs = node_value(row_points, 2 * row_count + 1)
    alt_acts = (1 - 2 * (jnp.arange(act_blocks) % 2)).astype(jnp.float32)
    alt_errs = (1 - 2 * (jnp.arange(err_blocks) % 2)).astype(jnp.float32)
    full_acts = lax.all_gather(hidden_acts, "col", axis=1, tiled=True)
    own_node = lax.dynamic_slice_in_dim(work_acts, col_place, 1, 0)
    encode_own = berrut(data_acts, alt_acts, jnp.ones((act_blocks,), jnp.float32), own_node)[:, 0]
    coded_acts = encode_blocks(full_acts, encode_own, act_blocks, act_width)
    full_errs = lax.all_gather(output_errors, "row", axis=1, tiled=True)
    own_err = lax.dynamic_slice_in_dim(work_errs, row_place, 1, 0)
    encode_err = berrut(data_errs, alt_errs, jnp.ones((err_blocks,), jnp.float32), own_err)[:, 0]
    coded_errs = encode_blocks(full_errs, encode_err, err_blocks, err_width)
    all_errs = lax.all_gather(coded_errs, "col", axis=0, tiled=True)
    product = lax.dot_general(
        all_errs,
        lax.all_gather(coded_acts, "row", axis=0, tiled=True),
        (((0,), (0,)), ((), ())),
        preferred_element_type=jnp.float32,
    ).astype(jnp.bfloat16)
    live = lax.dynamic_slice_in_dim(worker_mask, row_place, 1, 0)[0]
    decode_acts = berrut(
        work_acts, rank_signs(col_points, live), live.astype(jnp.float32), data_acts
    )
    decoded = jnp.einsum(
        "jk,jrf->rkf",
        decode_acts,
        lax.all_to_all(product[None], "col", split_axis=1, concat_axis=0, tiled=True).astype(
            jnp.float32
        ),
    ).astype(jnp.bfloat16)
    decoded = decoded.reshape(decoded.shape[0], FF)
    all_rows = jnp.ones((row_count,), jnp.int32)
    decode_errs = berrut(
        work_errs, rank_signs(row_points, all_rows), jnp.ones((row_count,), jnp.float32), data_errs
    )
    grad = jnp.einsum(
        "il,irf->lrf",
        decode_errs,
        lax.all_to_all(decoded[None], "row", split_axis=2, concat_axis=0, tiled=True).astype(
            jnp.float32
        ),
    )
    squares = lax.psum(jnp.sum(grad * grad), ("row", "col"))
    factor = jnp.minimum(1.0, jnp.sqrt(jnp.float32(FF * D)) / jnp.sqrt(squares + 1e-06))
    return grad * factor


def solution(mesh):
    return jax.shard_map(
        shards,
        mesh=mesh,
        in_specs=(P("row", "col"), P("col", "row"), P(), P(), P()),
        out_specs=P(None, "col", "row"),
        check_vma=False,
    )
```

profile of v0, /device:TPU:12, one launch (start us, length us, event | category | flops | bytes accessed | tf_op | source)
XLA Modules:
  0.0 2220.5 jit_solution(384368010853941417)
XLA Ops:
  6.5 0.7 all-gather.9.cloned.1.call-update
  7.3 0.7 multiply_cosine_fusion.2
  8.0 0.6 dynamic_slice.37
  8.7 1.3 divide_reduce_fusion.1
  10.0 6.0 all_gather.12
  15.9 1.3 multiply_divide_fusion.1
  17.2 2.7 while.28
  17.9 0.7 select_add_fusion.4
  19.2 0.7 select_add_fusion.4
  20.0 0.7 convert_element_type.111
  20.7 0.7 dynamic-slice_bitcast_fusion
  21.4 0.9 select_reduce_fusion
  22.3 0.7 fusion.27
  23.6 1.4 divide_reduce_fusion
  25.0 1.3 multiply_divide_fusion
  26.3 52.1 %all-gather.9.cloned.1.call-done = bf16[8,3696,64]{1,2,0:T(8,128)(2,1)} async-done(((bf16[1,3696,64]{1,2,0:T(8,128)(2,1)}), bf16[8,3696,64]{1,2,0:T(8,128)(2,1)}) %all-gather.9.cloned.1.call-update) | async-done | bytes 3784720 | tf_op jit(solution)/shard_map/all_gather | solution.py:53
  78.4 6.1 copy.25
  84.5 6.5 reshape.100
  90.9 12.4 while.29
  91.5 2.5 select_add_fusion.5
  94.6 2.5 select_add_fusion.5
  97.7 2.5 select_add_fusion.5
  100.8 2.5 select_add_fusion.5
  103.3 1.0 convert_element_type.115
  104.4 14.1 all-gather.5.cloned.1.call-done
  118.5 32.8 %all-gather.7.cloned.1.call-done = bf16[256,7392]{1,0:T(8,128)(2,1)} async-done(((bf16[64,7392]{1,0:T(8,128)(2,1)}), bf16[256,7392]{1,0:T(8,128)(2,1)}) %all-gather.7.cloned.1.call-update) | async-done | bytes 3784720 | tf_op jit(solution)/shard_map/all_gather | solution.py:64
  151.3 15.0 convert_bitcast_fusion
  166.2 123.4 %copy.26 = bf16[1,2048,7392]{2,0,1:T(2,128)(2,1)} copy(bf16[1,2048,7392]{1,2,0:T(8,128)(2,1)} %convert_bitcast_fusion) | data formatting | bytes 60555264 | tf_op jit(solution)/shard_map/broadcast_in_dim | solution.py:75
  290.1 188.5 %reduce.2 = bf16[2048,7392]{1,0:T(8,128)(2,1)} reduce(bf16[2048,1,7392]{2,1,0:T(2,128)(2,1)} %bitcast.51, bf16[]{:T(256)} %broadcast.331), dimensions={1}, to_apply=%bitcast.30.reduce_sub_computation | reduce | bytes 60555264
  478.6 48.8 %reshape.104 = bf16[8,2,946176]{2,1,0:T(2,128)(2,1)} reshape(bf16[2048,7392]{1,0:T(8,128)(2,1)} %reduce.2) | data formatting | bytes 60555264
  527.4 7.2 all-to-all-start
  534.8 650.3 %all-to-all-done = bf16[8,2,946176]{2,1,0:T(2,128)(2,1)} async-done(((bf16[8,2,946176]{2,1,0:T(2,128)(2,1)}), bf16[8,2,946176]{2,1,0:T(2,128)(2,1)}, u32[]{:S(2)}, u32[]{:S(2)}) %all-to-all-start) | async-done | bytes 30277664 | tf_op jit(solution)/shard_map/all_to_all | solution.py:75
  1185.1 86.2 %reshape.105 = bf16[2048,1,7392]{2,1,0:T(2,128)(2,1)} reshape(bf16[8,2,946176]{2,1,0:T(2,128)(2,1)} %all-to-all-done) | data formatting | bytes 60555264
  1271.3 30.4 %copy.33 = bf16[1,2048,7392]{2,1,0:T(8,128)(2,1)} copy(bf16[1,2048,7392]{2,0,1:T(2,128)(2,1)} %bitcast.52) | data formatting | bytes 60555264
  1301.7 39.8 %copy.32 = bf16[8,256,7392]{1,0,2:T(8,128)(2,1)} copy(bf16[8,256,7392]{2,1,0:T(8,128)(2,1)} %bitcast.53) | data formatting | bytes 60555264 | tf_op jit(solution)/shard_map/all_to_all | solution.py:75
  1341.5 17.5 convert_bitcast_fusion.1
  1358.9 9.0 copy.28
  1367.9 177.1 %copy.42 = bf16[1,256,29568]{1,0,2:T(2,128)(2,1)} copy(bf16[1,256,29568]{1,2,0:T(8,128)(2,1)S(1)} %bitcast.56) | data formatting | bytes 30277632 | tf_op jit(solution)/shard_map/broadcast_in_dim;reshape | solution.py:87
  1545.0 322.2 %reduce.3 = bf16[29568,256]{1,0:T(8,128)(2,1)} reduce(bf16[29568,1,256]{2,1,0:T(2,128)(2,1)} %bitcast.54, bf16[]{:T(256)} %broadcast.331), dimensions={1}, to_apply=%bitcast.44.reduce_sub_computation | reduce | bytes 30277634
  1867.2 12.0 reshape.106
  1879.2 8.4 all-to-all-start.1
  1888.0 163.4 %all-to-all-done.1 = bf16[4,2,946176]{2,1,0:T(2,128)(2,1)} async-done(((bf16[4,2,946176]{2,1,0:T(2,128)(2,1)}), bf16[4,2,946176]{2,1,0:T(2,128)(2,1)}, u32[]{:S(2)}, u32[]{:S(2)}) %all-to-all-start.1) | async-done | bytes 15138848 | tf_op jit(solution)/shard_map/all_to_all | solution.py:87
  2051.4 33.1 %reshape.107 = bf16[29568,1,256]{2,1,0:T(2,128)(2,1)} reshape(bf16[4,2,946176]{2,1,0:T(2,128)(2,1)} %all-to-all-done.1) | data formatting | bytes 30277632
  2084.5 18.8 copy.34
  2103.3 44.4 %multiply_reduce_fusion = (f32[]{:T(128)}, f32[2,256,7392]{1,0,2:T(2,128)}) fusion(bf16[1,256,4,7392]{1,3,2,0:T(8,128)(2,1)} %bitcast.59, f32[2]{0:T(128)S(1)} %fusion.7, f32[4]{0:T(128)S(1)} %copy-done.1, f32[4]{0:T(128)S(1)} %fusion.17, f32[2]{0:T(128)S(1)} %multiply_cosine_fusion.3), kind=kOutput, calls=%fused_computation.6 | convolution fusion | flops 37847064 | bytes 30277684 | tf_op jit(solution)/shard_map/il,irf->lrf/dot_general | solution.py:84
  2147.7 42.6 %psum.7 = f32[]{:T(128)} all-reduce(f32[]{:T(128)} %get-tuple-element.211), channel_id=1, replica_groups=mesh['row'=4,'col'=8] {'row','col'}, use_global_device_ids=true, to_apply=%region_11.12 | all-reduce | flops 1 | bytes 8 | tf_op jit(solution)/shard_map/psum | solution.py:91
  2191.0 10.6 broadcast_multiply_fusion
  2201.6 12.1 copy.31
  (27 shorter events, 5.5 us)
Async XLA Ops:
  6.5 71.9 %all-gather.9.cloned.1.call-start = ((), (), s32[]{:S(2)}) async-start(), calls=%async_computation.4 | async-start | bytes 4276224 | tf_op jit(solution)/shard_map/all_gather | solution.py:53
  7.3 111.2 %all-gather.5.cloned.1.call-start = ((), (), s32[]{:S(2)}) async-start(), calls=%async_computation.2 | async-start | bytes 1179648 | tf_op jit(solution)/shard_map/all_gather | solution.py:61
  8.0 0.7 copy-start
  20.6 130.6 %all-gather.7.cloned.1.call-start = ((), (), s32[]{:S(2)}) async-start(), calls=%async_computation.3 | async-start | bytes 4751360 | tf_op jit(solution)/shard_map/all_gather | solution.py:64
  527.4 657.6 %all-to-all-start = ((bf16[8,2,946176]{2,1,0:T(2,128)(2,1)}), bf16[8,2,946176]{2,1,0:T(2,128)(2,1)}, u32[]{:S(2)}, u32[]{:S(2)}) async-start(bf16[8,2,946176]{2,1,0:T(2,128)(2,1)} %reshape.104), calls=%async_computation | async-start | bytes 60555264 | tf_op jit(solution)/shard_map/all_to_all | solution.py:75
  1879.2 8.5 copy-start.2
  1879.2 8.7 copy-start.1
  1879.2 172.3 %all-to-all-start.1 = ((bf16[4,2,946176]{2,1,0:T(2,128)(2,1)}), bf16[4,2,946176]{2,1,0:T(2,128)(2,1)}, u32[]{:S(2)}, u32[]{:S(2)}) async-start(bf16[4,2,946176]{2,1,0:T(2,128)(2,1)} %reshape.106), calls=%async_computation.1 | async-start | bytes 30277632 | tf_op jit(solution)/shard_map/all_to_all | solution.py:87
Sparse Core Ops, SparseCore 0:
  9.5 68.8 all-gather.8
  80.5 37.9 all-gather.4
  120.1 31.1 all-gather.6
where the time goes:
time: 2230 us; the launch traced here: 2220 us
  waiting for transfers between devices  913 us (41%)
  local copies, waits for them, and re-layouts  609 us (27%)
  other arithmetic  543 us (24%)
  matrix products  76.8 us (3%)
  blocking collectives  48.6 us (2%)
    all_to_all x1, waiting for transfers between devices, shards(): lax.all_to_all(product[None], 'col', split_axis=1, concat_axis=0, tiled=T...  650 us
    unnamed x4, other arithmetic  511 us
    unnamed x14, local copies, waits for them, and re-layouts  236 us
    another operation x1, local copies, waits for them, and re-layouts, shards(): decoded[None]  177 us
    all_to_all x1, waiting for transfers between devices, shards(): lax.all_to_all(decoded[None], 'row', split_axis=2, concat_axis=0, tiled=T...  163 us
    broadcast_in_dim x1, local copies, waits for them, and re-layouts, shards(): product[None]  123 us
    all_gather x1, waiting for transfers between devices, shards(): full_acts = lax.all_gather(hidden_acts, 'col', axis=1, tiled=True)  52.1 us
  transfers between devices with their start and end apart: 5, of which 5 were waited for; matrix products, arithmetic and copies ran while one was open for 2% of the time, Pallas kernels for 0%

commit v1 on v0

--- a/solution.py
+++ b/solution.py
@@ -72,9 +72,12 @@
     decoded = jnp.einsum(
         "jk,jrf->rkf",
         decode_acts,
-        lax.all_to_all(product[None], "col", split_axis=1, concat_axis=0, tiled=True).astype(
-            jnp.float32
-        ),
+        jnp.concatenate(
+            lax.all_to_all(
+                jnp.stack(jnp.split(product[None], lax.axis_size("col"), axis=1)), "col", 0, 0
+            ),
+            axis=0,
+        ).astype(jnp.float32),
     ).astype(jnp.bfloat16)
     decoded = decoded.reshape(decoded.shape[0], FF)
     all_rows = jnp.ones((row_count,), jnp.int32)

time: 2230 us -> 1790 us (0.80)
  local copies, waits for them, and re-layouts: 609 us -> 313 us
  other arithmetic: 543 us -> 354 us
  matrix products: 76.8 us -> 120 us
    unnamed x4 -> x3, other arithmetic: 511 us -> 323 us
    unnamed x14 -> x18, local copies, waits for them, and re-layouts: 236 us -> 99.7 us
    broadcast_in_dim x1 -> x0, local copies, waits for them, and re-layouts: 123 us -> none  [shards(): product[None]]
    dot_general x1, matrix products: 17.5 us -> 60.5 us  [shards(): jnp.einsum('jk,jrf->rkf', decode_acts, jnp.concatenate(lax.all_to_all(jnp...]
    all_to_all x1 -> x0, local copies, waits for them, and re-layouts: 39.8 us -> none  [shards(): lax.all_to_all(product[None], 'col', split_axis=1, concat_axis=0, tiled=T...]
where the time goes in v1:
time: 1790 us; the launch traced here: 1780 us
  waiting for transfers between devices  915 us (51%)
  other arithmetic  354 us (20%)
  local copies, waits for them, and re-layouts  313 us (17%)
  matrix products  120 us (7%)
  blocking collectives  48.6 us (3%)
    all_to_all x1, waiting for transfers between devices, shards(): lax.all_to_all(jnp.stack(jnp.split(product[None], lax.axis_size('col'), a...  650 us
    unnamed x3, other arithmetic  323 us
    another operation x1, local copies, waits for them, and re-layouts, shards(): decoded[None]  177 us
    all_to_all x1, waiting for transfers between devices, shards(): lax.all_to_all(decoded[None], 'row', split_axis=2, concat_axis=0, tiled=T...  163 us
    unnamed x18, local copies, waits for them, and re-layouts  99.7 us
    dot_general x1, matrix products, shards(): jnp.einsum('jk,jrf->rkf', decode_acts, jnp.concatenate(lax.all_to_all(jnp...  60.5 us
    all_gather x1, waiting for transfers between devices, shards(): full_acts = lax.all_gather(hidden_acts, 'col', axis=1, tiled=True)  53.8 us
    dot_general x1, matrix products, shards(): jnp.einsum('il,irf->lrf', decode_errs, lax.all_to_all(decoded[None], 'row...  44.4 us
  transfers between devices with their start and end apart: 5, of which 5 were waited for; matrix products, arithmetic and copies ran while one was open for 2% of the time, Pallas kernels for 0%

profile of v1, /device:TPU:12, one launch (start us, length us, event | category | flops | bytes accessed | tf_op | source)
XLA Modules:
  0.0 1779.6 jit_solution(11976807938782614702)
XLA Ops:
  6.5 0.7 all-gather.9.cloned.1.call-update
  7.3 0.7 multiply_cosine_fusion.2
  8.0 0.6 dynamic_slice.37
  8.7 1.3 divide_reduce_fusion.1
  9.9 6.0 all_gather.12
  15.9 1.3 multiply_divide_fusion.1
  17.2 2.7 while.28
  17.9 0.7 select_add_fusion.4
  19.2 0.7 select_add_fusion.4
  19.9 0.7 convert_element_type.111
  20.7 0.7 multiply_cosine_fusion.1
  22.0 1.3 divide_reduce_fusion
  23.3 1.3 multiply_divide_fusion
  24.6 53.8 %all-gather.9.cloned.1.call-done = bf16[8,3696,64]{1,2,0:T(8,128)(2,1)} async-done(((bf16[1,3696,64]{1,2,0:T(8,128)(2,1)}), bf16[8,3696,64]{1,2,0:T(8,128)(2,1)}) %all-gather.9.cloned.1.call-update) | async-done | bytes 3784720 | tf_op jit(solution)/shard_map/all_gather | solution.py:53
  78.4 6.1 copy.25
  84.5 6.3 reshape.101
  90.8 12.4 while.29
  91.4 2.5 select_add_fusion.5
  94.5 2.5 select_add_fusion.5
  97.6 2.5 select_add_fusion.5
  100.7 2.5 select_add_fusion.5
  103.2 1.0 convert_element_type.115
  104.2 14.2 all-gather.5.cloned.1.call-done
  118.5 32.8 %all-gather.7.cloned.1.call-done = bf16[256,7392]{1,0:T(8,128)(2,1)} async-done(((bf16[64,7392]{1,0:T(8,128)(2,1)}), bf16[256,7392]{1,0:T(8,128)(2,1)}) %all-gather.7.cloned.1.call-update) | async-done | bytes 3784720 | tf_op jit(solution)/shard_map/all_gather | solution.py:64
  151.2 15.1 convert_bitcast_fusion
  166.3 4.2 fusion.14
  170.5 4.2 fusion.13
  174.7 4.1 fusion.12
  178.8 4.2 fusion.11
  183.0 4.2 fusion.10
  187.2 4.1 fusion.9
  191.3 4.1 fusion.8
  195.4 4.2 fusion.7
  199.6 7.2 all-to-all-start
  207.2 650.0 %all-to-all-done = bf16[8,1,256,7392]{2,3,1,0:T(8,128)(2,1)} async-done(((bf16[8,1,256,7392]{2,3,1,0:T(8,128)(2,1)}), bf16[8,1,256,7392]{2,3,1,0:T(8,128)(2,1)}, u32[]{:S(2)}, u32[]{:S(2)}) %all-to-all-start) | async-done | bytes 30277664 | tf_op jit(solution)/shard_map/all_to_all | solution.py:76
  857.2 60.5 %convert_bitcast_fusion.1 = bf16[256,4,7392]{0,1,2:T(4,128)(2,1)} fusion(bf16[8,256,7392]{1,2,0:T(8,128)(2,1)} %bitcast.15, f32[4]{0:T(128)S(1)} %fusion.15, f32[8]{0:T(128)S(1)} %multiply_cosine_fusion.1, f32[4]{0:T(128)S(1)} %multiply_cosine_fusion, f32[8]{0:T(128)S(1)} %fusion.39), kind=kOutput, calls=%fused_computation.9 | convolution fusion | flops 128680032 | bytes 45416544 | tf_op jit(solution)/shard_map/jk,jrf->rkf/dot_general | solution.py:72
  917.7 9.0 copy.27
  926.7 176.7 %copy.43 = bf16[1,256,29568]{1,0,2:T(2,128)(2,1)} copy(bf16[1,256,29568]{1,2,0:T(8,128)(2,1)S(1)} %bitcast.82) | data formatting | bytes 30277632 | tf_op jit(solution)/shard_map/broadcast_in_dim;reshape | solution.py:90
  1103.8 322.6 %reduce.2 = bf16[29568,256]{1,0:T(8,128)(2,1)} reduce(bf16[29568,1,256]{2,1,0:T(2,128)(2,1)} %bitcast.80, bf16[]{:T(256)} %broadcast.331), dimensions={1}, to_apply=%bitcast.73.reduce_sub_computation | reduce | bytes 30277634
  1426.4 11.8 reshape.104
  1438.3 8.5 all-to-all-start.1
  1447.2 163.4 %all-to-all-done.1 = bf16[4,2,946176]{2,1,0:T(2,128)(2,1)} async-done(((bf16[4,2,946176]{2,1,0:T(2,128)(2,1)}), bf16[4,2,946176]{2,1,0:T(2,128)(2,1)}, u32[]{:S(2)}, u32[]{:S(2)}) %all-to-all-start.1) | async-done | bytes 15138848 | tf_op jit(solution)/shard_map/all_to_all | solution.py:90
  1610.6 33.1 %reshape.105 = bf16[29568,1,256]{2,1,0:T(2,128)(2,1)} reshape(bf16[4,2,946176]{2,1,0:T(2,128)(2,1)} %all-to-all-done.1) | data formatting | bytes 30277632
  1643.7 18.8 %copy.31 = bf16[1,256,29568]{1,2,0:T(8,128)(2,1)} copy(bf16[1,256,29568]{1,0,2:T(2,128)(2,1)} %bitcast.81) | data formatting | bytes 30277632
  1662.5 44.4 %multiply_reduce_fusion = (f32[]{:T(128)}, f32[2,256,7392]{1,0,2:T(2,128)}) fusion(bf16[1,256,4,7392]{1,3,2,0:T(8,128)(2,1)} %bitcast.85, f32[2]{0:T(128)S(1)} %fusion.19, f32[4]{0:T(128)S(1)} %multiply_cosine_fusion.2, f32[4]{0:T(128)S(1)} %fusion.29, f32[2]{0:T(128)S(1)} %multiply_cosine_fusion.3), kind=kOutput, calls=%fused_computation.8 | convolution fusion | flops 37847064 | bytes 30277684 | tf_op jit(solution)/shard_map/il,irf->lrf/dot_general | solution.py:87
  1706.9 42.6 %psum.7 = f32[]{:T(128)} all-reduce(f32[]{:T(128)} %get-tuple-element.211), channel_id=1, replica_groups=mesh['row'=4,'col'=8] {'row','col'}, use_global_device_ids=true, to_apply=%region_11.12 | all-reduce | flops 1 | bytes 8 | tf_op jit(solution)/shard_map/psum | solution.py:94
  1750.2 10.6 broadcast_multiply_fusion
  1760.8 12.1 copy.30
  (30 shorter events, 5.7 us)
Async XLA Ops:
  6.5 71.9 %all-gather.9.cloned.1.call-start = ((), (), s32[]{:S(2)}) async-start(), calls=%async_computation.4 | async-start | bytes 4276224 | tf_op jit(solution)/shard_map/all_gather | solution.py:53
  7.3 111.2 %all-gather.5.cloned.1.call-start = ((), (), s32[]{:S(2)}) async-start(), calls=%async_computation.2 | async-start | bytes 1179648 | tf_op jit(solution)/shard_map/all_gather | solution.py:61
  20.6 130.6 %all-gather.7.cloned.1.call-start = ((), (), s32[]{:S(2)}) async-start(), calls=%async_computation.3 | async-start | bytes 4751360 | tf_op jit(solution)/shard_map/all_gather | solution.py:64
  199.6 7.2 copy-start.1
  199.6 7.2 copy-start
  199.6 657.6 %all-to-all-start = ((bf16[8,1,256,7392]{2,3,1,0:T(8,128)(2,1)}), bf16[8,1,256,7392]{2,3,1,0:T(8,128)(2,1)}, u32[]{:S(2)}, u32[]{:S(2)}) async-start(bf16[8,1,256,7392]{2,3,1,0:T(8,128)(2,1)} %fusion.7), calls=%async_computation | async-start | bytes 60555264 | tf_op jit(solution)/shard_map/all_to_all | solution.py:76
  1438.3 8.5 copy-start.2
  1438.3 172.3 %all-to-all-start.1 = ((bf16[4,2,946176]{2,1,0:T(2,128)(2,1)}), bf16[4,2,946176]{2,1,0:T(2,128)(2,1)}, u32[]{:S(2)}, u32[]{:S(2)}) async-start(bf16[4,2,946176]{2,1,0:T(2,128)(2,1)} %reshape.104), calls=%async_computation.1 | async-start | bytes 30277632 | tf_op jit(solution)/shard_map/all_to_all | solution.py:90
Sparse Core Ops, SparseCore 0:
  9.5 68.8 all-gather.8
  80.5 37.8 all-gather.4
  120.0 31.1 all-gather.6
